TPU v7x, 8 devices: a whole 2x2x1 slice. The times are simulated.
8 devices in a mesh: batch: 1 (over z), col: 2 (over y), row: 4 (over x, core).
Axes of the slice: x: 2, y: 2, z: 1, core: 2. Of those that a mesh axis runs over, the one named last changes fastest.
Arguments:
- d_inv: bfloat16 [24, 1024, 1024], P(('batch', 'row'))
- l_blk: bfloat16 [24, 1024, 1024], P(('batch', 'row'))
- u_blk: bfloat16 [24, 1024, 1024], P(('batch', 'row'))
- rhs_blk: float32 [24, 1024, 256], P(('batch', 'row'), None, 'col')
- x_init: float32 [24, 1024, 256], P(('batch', 'row'), None, 'col')
Outputs:
- output: float32 [24, 1024, 256], P(('batch', 'row'), None, 'col')
All inputs are finite; a program needn't handle non-finite values.
Results may differ from a plain program's by a relative error of at most 0.0111632.
Values are sent between devices in bfloat16 or wider.
A program may use at most 1 GiB of HBM per device.

v0:
```python
import jax
import jax.numpy as jnp
from jax import lax
from jax.sharding import PartitionSpec as P

SWEEPS = 4


def row_step(x_left, row_in):
    d_i, l_i, u_i, f_i, x_right = row_in
    t_i = (f_i
           - jnp.dot(l_i, x_left.astype(jnp.bfloat16), preferred_element_type=jnp.float32)
           - jnp.dot(u_i, x_right.astype(jnp.bfloat16), preferred_element_type=jnp.float32))
    x_i = jnp.dot(d_i, t_i.astype(jnp.bfloat16), preferred_element_type=jnp.float32)
    return x_i, x_i


def solution(mesh):
    chain_len = mesh.shape["row"]
    mat_spec = P(("batch", "row"), None, None)
    vec_spec = P(("batch", "row"), None, "col")
    fwd_perm = [(src_dev, src_dev + 1) for src_dev in range(chain_len - 1)]
    back_perm = [(src_dev + 1, src_dev) for src_dev in range(chain_len - 1)]

    def device_fn(d_inv, l_blk, u_blk, rhs_blk, x_init):
        chain_pos = lax.axis_index("row")
        zero_blk = jnp.zeros(x_init.shape[1:], jnp.float32)
        x_cur = x_init
        for sweep_idx in range(SWEEPS):
            from_right = lax.ppermute(x_cur[0], "row", back_perm)
            x_right = jnp.concatenate([x_cur[1:], from_right[None]], axis=0)

            def local_sweep(x_left, x_right=x_right):
                _, x_new = lax.scan(row_step, x_left, (d_inv, l_blk, u_blk, rhs_blk, x_right))
                return x_new

            def run_stage(stage_idx, stage_state, local_sweep=local_sweep):
                x_run, x_left = stage_state
                x_run = lax.cond(chain_pos == stage_idx, lambda: local_sweep(x_left), lambda: x_run)
                x_left = lax.ppermute(x_run[-1], "row", fwd_perm)
                return x_run, x_left

            x_cur, _ = lax.fori_loop(0, chain_len, run_stage, (x_cur, zero_blk))
        return x_cur

    return jax.shard_map(device_fn, mesh=mesh, in_specs=(mat_spec, mat_spec, mat_spec, vec_spec, vec_spec), out_specs=vec_spec, check_vma=False)
```

profile of v0, /device:TPU:7, one launch (start us, length us, event | category | flops | bytes accessed | tf_op | source)
XLA Modules:
  0.0 718.2 jit_solution(14469935670767971554)
XLA Ops:
  1.9 2.6 collective-permute-start.4
  7.3 203.0 %while.120 = (s32[]{:T(128)}, f32[6,1024,128]{2,1,0:T(8,128)}, bf16[1024,128]{1,0:T(8,128)(2,1)S(1)}, s32[]{:T(128)}, bf16[6,1024,1024]{2,1,0:T(8,128)(2,1)}, /*...) while((s32[]{:T(128)}, f32[6,1024,128]{2,1,0:T(8,128)}, ...), condition=%wide.region_5.6_spmd, body=%wide.region_0.5_spmd.sunk | while | flops 805830656 | bytes 10751360 | solution.py:43
  9.7 4.2 collective-permute-done.3
  16.3 6.6 collective-permute-done.3
  25.3 134.8 %collective-permute-done.3 = bf16[1024,128]{1,0:T(8,128)(2,1)S(1)} collective-permute-done((bf16[1024,128]{1,0:T(8,128)(2,1)S(1)}, bf16[1024,128]{1,0:T(8,128)(2,1)S(1)}, u32[]{:S(2)}, u32[]{:S(2)}) %collective-permute-start.3) | collective-permute-done | bytes 262176 | tf_op jit(solution)/shard_map/while/body/eval_jaxpr/ppermute | solution.py:40
  160.0 45.8 %conditional.8 = (f32[6,1024,128]{2,1,0:T(8,128)}) conditional(s32[]{:T(128)} %convert_element_type.132, f32[6,1024,128]{2,1,0:T(8,128)} %get-tuple-element.1600, (bf16[6,1024,1024]{2,1,0:T(8,128)(2,1)}, f32[6,1024,128]{2,1,0:T(8,128)}, bf16[6,1024,1024]{2,1,0:T(8,128)(2,1)}, bf16[6,1024,1024]{2,1,0:T(8,128)(2,1)}, ...), branch_computations={%region_1.0_spmd, %region_2.4_spmd} | conditional | flops 805830656 | bytes 9178293 | solution.py:39
  160.0 45.8 %while.116 = (s32[]{:T(128)}, bf16[1024,128]{1,0:T(8,128)(2,1)S(1)}, f32[6,1024,128]{2,1,0:T(8,128)}, bf16[6,1024,1024]{2,1,0:T(8,128)(2,1)}, f32[6,1024,128]{2,...) while((s32[]{:T(128)}, bf16[1024,128]{1,0:T(8,128)(2,1)S(1)}, ...), condition=%wide.region_4.3_spmd, body=%wide.region_3.2_spmd.sunk | while | flops 805830656 | bytes 9178205 | solution.py:34
  160.0 2.4 fusion.167
  162.4 5.2 bitcast_dynamic-update-slice_fusion.11
  167.7 2.4 fusion.167
  170.0 5.2 bitcast_dynamic-update-slice_fusion.11
  175.3 2.4 fusion.167
  177.7 5.2 bitcast_dynamic-update-slice_fusion.11
  182.9 2.4 fusion.167
  185.3 5.2 bitcast_dynamic-update-slice_fusion.11
  192.9 5.2 bitcast_dynamic-update-slice_fusion.11
  198.2 2.4 fusion.167
  200.6 5.2 bitcast_dynamic-update-slice_fusion.11
  215.6 164.1 %while.121 = (s32[]{:T(128)}, f32[6,1024,128]{2,1,0:T(8,128)}, bf16[1024,128]{1,0:T(8,128)(2,1)S(1)}, s32[]{:T(128)}, bf16[6,1024,1024]{2,1,0:T(8,128)(2,1)}, /*...) while((s32[]{:T(128)}, f32[6,1024,128]{2,1,0:T(8,128)}, ...), condition=%wide.region_11.12_spmd, body=%wide.region_6.11_spmd.sunk | while | flops 805830656 | bytes 10751360 | solution.py:43
  218.0 3.5 collective-permute-done.2
  223.9 6.6 collective-permute-done.2
  232.9 96.5 %collective-permute-done.2 = bf16[1024,128]{1,0:T(8,128)(2,1)S(1)} collective-permute-done((bf16[1024,128]{1,0:T(8,128)(2,1)S(1)}, bf16[1024,128]{1,0:T(8,128)(2,1)S(1)}, u32[]{:S(2)}, u32[]{:S(2)}) %collective-permute-start.2) | collective-permute-done | bytes 262176 | tf_op jit(solution)/shard_map/while/body/eval_jaxpr/ppermute | solution.py:40
  329.3 45.8 %conditional.9 = (f32[6,1024,128]{2,1,0:T(8,128)}) conditional(s32[]{:T(128)} %convert_element_type.133, f32[6,1024,128]{2,1,0:T(8,128)} %get-tuple-element.1630, (bf16[6,1024,1024]{2,1,0:T(8,128)(2,1)}, f32[6,1024,128]{2,1,0:T(8,128)}, bf16[6,1024,1024]{2,1,0:T(8,128)(2,1)}, bf16[6,1024,1024]{2,1,0:T(8,128)(2,1)}, ...), branch_computations={%region_7.7_spmd, %region_8.10_spmd} | conditional | flops 805830656 | bytes 9178293 | solution.py:39
  329.3 45.8 %while.117 = (s32[]{:T(128)}, bf16[1024,128]{1,0:T(8,128)(2,1)S(1)}, f32[6,1024,128]{2,1,0:T(8,128)}, bf16[6,1024,1024]{2,1,0:T(8,128)(2,1)}, f32[6,1024,128]{2,...) while((s32[]{:T(128)}, bf16[1024,128]{1,0:T(8,128)(2,1)S(1)}, ...), condition=%wide.region_10.9_spmd, body=%wide.region_9.8_spmd.sunk | while | flops 805830656 | bytes 9178205 | solution.py:34
  331.7 5.2 bitcast_dynamic-update-slice_fusion.10
  337.0 2.4 fusion.162
  339.3 5.2 bitcast_dynamic-update-slice_fusion.10
  347.0 5.2 bitcast_dynamic-update-slice_fusion.10
  352.2 2.4 fusion.162
  354.6 5.2 bitcast_dynamic-update-slice_fusion.10
  362.2 5.2 bitcast_dynamic-update-slice_fusion.10
  367.5 2.4 fusion.162
  369.9 5.2 bitcast_dynamic-update-slice_fusion.10
  384.9 164.1 %while.122 = (s32[]{:T(128)}, f32[6,1024,128]{2,1,0:T(8,128)}, bf16[1024,128]{1,0:T(8,128)(2,1)S(1)}, s32[]{:T(128)}, bf16[6,1024,1024]{2,1,0:T(8,128)(2,1)}, /*...) while((s32[]{:T(128)}, f32[6,1024,128]{2,1,0:T(8,128)}, ...), condition=%wide.region_17.18_spmd, body=%wide.region_12.17_spmd.sunk | while | flops 805830656 | bytes 10751360 | solution.py:43
  387.3 3.5 collective-permute-done.1
  393.2 6.6 collective-permute-done.1
  402.2 96.5 %collective-permute-done.1 = bf16[1024,128]{1,0:T(8,128)(2,1)S(1)} collective-permute-done((bf16[1024,128]{1,0:T(8,128)(2,1)S(1)}, bf16[1024,128]{1,0:T(8,128)(2,1)S(1)}, u32[]{:S(2)}, u32[]{:S(2)}) %collective-permute-start.1) | collective-permute-done | bytes 262176 | tf_op jit(solution)/shard_map/while/body/eval_jaxpr/ppermute | solution.py:40
  498.6 45.8 %conditional.10 = (f32[6,1024,128]{2,1,0:T(8,128)}) conditional(s32[]{:T(128)} %convert_element_type.134, f32[6,1024,128]{2,1,0:T(8,128)} %get-tuple-element.1660, (bf16[6,1024,1024]{2,1,0:T(8,128)(2,1)}, f32[6,1024,128]{2,1,0:T(8,128)}, bf16[6,1024,1024]{2,1,0:T(8,128)(2,1)}, bf16[6,1024,1024]{2,1,0:T(8,128)(2,1)}, ...), branch_computations={%region_13.13_spmd, %region_14.16_spmd} | conditional | flops 805830656 | bytes 9178293 | solution.py:39
  498.6 45.8 %while.118 = (s32[]{:T(128)}, bf16[1024,128]{1,0:T(8,128)(2,1)S(1)}, f32[6,1024,128]{2,1,0:T(8,128)}, bf16[6,1024,1024]{2,1,0:T(8,128)(2,1)}, f32[6,1024,128]{2,...) while((s32[]{:T(128)}, bf16[1024,128]{1,0:T(8,128)(2,1)S(1)}, ...), condition=%wide.region_16.15_spmd, body=%wide.region_15.14_spmd.sunk | while | flops 805830656 | bytes 9178205 | solution.py:34
  501.0 5.2 bitcast_dynamic-update-slice_fusion.9
  506.3 2.4 fusion.157
  508.6 5.2 bitcast_dynamic-update-slice_fusion.9
  516.3 5.2 bitcast_dynamic-update-slice_fusion.9
  521.5 2.4 fusion.157
  523.9 5.2 bitcast_dynamic-update-slice_fusion.9
  529.2 2.4 fusion.157
  531.5 5.2 bitcast_dynamic-update-slice_fusion.9
  536.8 2.4 fusion.157
  539.2 5.2 bitcast_dynamic-update-slice_fusion.9
  554.2 164.1 %while.123 = (s32[]{:T(128)}, f32[6,1024,128]{2,1,0:T(8,128)}, bf16[1024,128]{1,0:T(8,128)(2,1)S(1)}, s32[]{:T(128)}, bf16[6,1024,1024]{2,1,0:T(8,128)(2,1)}, /*...) while((s32[]{:T(128)}, f32[6,1024,128]{2,1,0:T(8,128)}, ...), condition=%wide.region_23.24_spmd, body=%wide.region_18.23_spmd.sunk | while | flops 805830656 | bytes 10751360 | solution.py:43
  556.6 3.5 collective-permute-done
  562.5 6.6 collective-permute-done
  571.5 96.5 %collective-permute-done = bf16[1024,128]{1,0:T(8,128)(2,1)S(1)} collective-permute-done((bf16[1024,128]{1,0:T(8,128)(2,1)S(1)}, bf16[1024,128]{1,0:T(8,128)(2,1)S(1)}, u32[]{:S(2)}, u32[]{:S(2)}) %collective-permute-start) | collective-permute-done | bytes 262176 | tf_op jit(solution)/shard_map/while/body/eval_jaxpr/ppermute | solution.py:40
  667.9 45.8 %conditional.11 = (f32[6,1024,128]{2,1,0:T(8,128)}) conditional(s32[]{:T(128)} %convert_element_type.135, f32[6,1024,128]{2,1,0:T(8,128)} %get-tuple-element.1690, (bf16[6,1024,1024]{2,1,0:T(8,128)(2,1)}, f32[6,1024,128]{2,1,0:T(8,128)}, bf16[6,1024,1024]{2,1,0:T(8,128)(2,1)}, bf16[6,1024,1024]{2,1,0:T(8,128)(2,1)}, ...), branch_computations={%region_19.19_spmd, %region_20.22_spmd} | conditional | flops 805830656 | bytes 9178293 | solution.py:39
  667.9 45.8 %while.119 = (s32[]{:T(128)}, bf16[1024,128]{1,0:T(8,128)(2,1)S(1)}, f32[6,1024,128]{2,1,0:T(8,128)}, bf16[6,1024,1024]{2,1,0:T(8,128)(2,1)}, f32[6,1024,128]{2,...) while((s32[]{:T(128)}, bf16[1024,128]{1,0:T(8,128)(2,1)S(1)}, ...), condition=%wide.region_22.21_spmd, body=%wide.region_21.20_spmd.sunk | while | flops 805830656 | bytes 9178205 | solution.py:34
  670.3 5.2 bitcast_dynamic-update-slice_fusion.8
  675.6 2.4 fusion.152
  677.9 5.2 bitcast_dynamic-update-slice_fusion.8
  685.6 5.2 bitcast_dynamic-update-slice_fusion.8
  690.8 2.4 fusion.152
  693.2 5.2 bitcast_dynamic-update-slice_fusion.8
  700.8 5.2 bitcast_dynamic-update-slice_fusion.8
  706.1 2.4 fusion.152
  708.5 5.2 bitcast_dynamic-update-slice_fusion.8
  (87 shorter events, 88.0 us)
Async XLA Ops:
  1.9 2.6 copy-start
  1.9 3.9 collective-permute-start.4
  8.4 5.5 collective-permute-start.3
  15.0 7.9 %collective-permute-start.3 = (bf16[1024,128]{1,0:T(8,128)(2,1)S(1)}, bf16[1024,128]{1,0:T(8,128)(2,1)S(1)}, u32[]{:S(2)}, u32[]{:S(2)}) collective-permute-start(bf16[1024,128]{1,0:T(8,128)(2,1)S(1)} %slice_bitcast_fusion.12), channel_id=1, source_target_pairs={{0,1},{1,2},{2,3},{4,5},{5,6},{6,7}} | collective-permute-start | bytes 786440 | tf_op jit(solution)/shard_map/while/body/eval_jaxpr/ppermute | solution.py:40
  24.0 136.1 %collective-permute-start.3 = (bf16[1024,128]{1,0:T(8,128)(2,1)S(1)}, bf16[1024,128]{1,0:T(8,128)(2,1)S(1)}, u32[]{:S(2)}, u32[]{:S(2)}) collective-permute-start(bf16[1024,128]{1,0:T(8,128)(2,1)S(1)} %slice_bitcast_fusion.12), channel_id=1, source_target_pairs={{0,1},{1,2},{2,3},{4,5},{5,6},{6,7}} | collective-permute-start | bytes 786440 | tf_op jit(solution)/shard_map/while/body/eval_jaxpr/ppermute | solution.py:40
  206.9 3.4 collective-permute-start.3
  211.4 4.0 collective-permute-start.5
  216.7 4.8 collective-permute-start.2
  222.6 7.9 %collective-permute-start.2 = (bf16[1024,128]{1,0:T(8,128)(2,1)S(1)}, bf16[1024,128]{1,0:T(8,128)(2,1)S(1)}, u32[]{:S(2)}, u32[]{:S(2)}) collective-permute-start(bf16[1024,128]{1,0:T(8,128)(2,1)S(1)} %slice_bitcast_fusion.13), channel_id=1, source_target_pairs={{0,1},{1,2},{2,3},{4,5},{5,6},{6,7}} | collective-permute-start | bytes 786440 | tf_op jit(solution)/shard_map/while/body/eval_jaxpr/ppermute | solution.py:40
  231.6 97.8 %collective-permute-start.2 = (bf16[1024,128]{1,0:T(8,128)(2,1)S(1)}, bf16[1024,128]{1,0:T(8,128)(2,1)S(1)}, u32[]{:S(2)}, u32[]{:S(2)}) collective-permute-start(bf16[1024,128]{1,0:T(8,128)(2,1)S(1)} %slice_bitcast_fusion.13), channel_id=1, source_target_pairs={{0,1},{1,2},{2,3},{4,5},{5,6},{6,7}} | collective-permute-start | bytes 786440 | tf_op jit(solution)/shard_map/while/body/eval_jaxpr/ppermute | solution.py:40
  376.2 3.4 collective-permute-start.2
  380.7 4.0 collective-permute-start.6
  386.0 4.8 collective-permute-start.1
  391.9 7.9 %collective-permute-start.1 = (bf16[1024,128]{1,0:T(8,128)(2,1)S(1)}, bf16[1024,128]{1,0:T(8,128)(2,1)S(1)}, u32[]{:S(2)}, u32[]{:S(2)}) collective-permute-start(bf16[1024,128]{1,0:T(8,128)(2,1)S(1)} %slice_bitcast_fusion.14), channel_id=1, source_target_pairs={{0,1},{1,2},{2,3},{4,5},{5,6},{6,7}} | collective-permute-start | bytes 786440 | tf_op jit(solution)/shard_map/while/body/eval_jaxpr/ppermute | solution.py:40
  400.9 97.8 %collective-permute-start.1 = (bf16[1024,128]{1,0:T(8,128)(2,1)S(1)}, bf16[1024,128]{1,0:T(8,128)(2,1)S(1)}, u32[]{:S(2)}, u32[]{:S(2)}) collective-permute-start(bf16[1024,128]{1,0:T(8,128)(2,1)S(1)} %slice_bitcast_fusion.14), channel_id=1, source_target_pairs={{0,1},{1,2},{2,3},{4,5},{5,6},{6,7}} | collective-permute-start | bytes 786440 | tf_op jit(solution)/shard_map/while/body/eval_jaxpr/ppermute | solution.py:40
  545.5 3.4 collective-permute-start.1
  550.0 4.0 collective-permute-start.7
  555.3 4.8 collective-permute-start
  561.2 7.9 %collective-permute-start = (bf16[1024,128]{1,0:T(8,128)(2,1)S(1)}, bf16[1024,128]{1,0:T(8,128)(2,1)S(1)}, u32[]{:S(2)}, u32[]{:S(2)}) collective-permute-start(bf16[1024,128]{1,0:T(8,128)(2,1)S(1)} %slice_bitcast_fusion.15), channel_id=1, source_target_pairs={{0,1},{1,2},{2,3},{4,5},{5,6},{6,7}} | collective-permute-start | bytes 786440 | tf_op jit(solution)/shard_map/while/body/eval_jaxpr/ppermute | solution.py:40
  570.2 97.8 %collective-permute-start = (bf16[1024,128]{1,0:T(8,128)(2,1)S(1)}, bf16[1024,128]{1,0:T(8,128)(2,1)S(1)}, u32[]{:S(2)}, u32[]{:S(2)}) collective-permute-start(bf16[1024,128]{1,0:T(8,128)(2,1)S(1)} %slice_bitcast_fusion.15), channel_id=1, source_target_pairs={{0,1},{1,2},{2,3},{4,5},{5,6},{6,7}} | collective-permute-start | bytes 786440 | tf_op jit(solution)/shard_map/while/body/eval_jaxpr/ppermute | solution.py:40
  714.8 3.4 collective-permute-start
where the time goes:
time: 721 us; the launch traced here: 718 us
  waiting for transfers between devices  474 us (66%)
  matrix products  183 us (25%)
  local copies, waits for them, and re-layouts  29.4 us (4%)
  starting transfers between devices  29.4 us (4%)
    ppermute x16, waiting for transfers between devices, run_stage(): x_left = lax.ppermute(x_run[-1], 'row', fwd_perm)  474 us
    dot_general x24, matrix products, row_step(): jnp.dot(d_i, t_i.astype(jnp.bfloat16), preferred_element_type=jnp.float32)  126 us
    dot_general x24, matrix products, row_step(): jnp.dot(l_i, x_left.astype(jnp.bfloat16), preferred_element_type=jnp.floa...  57 us
    ppermute x16, starting transfers between devices, run_stage(): x_left = lax.ppermute(x_run[-1], 'row', fwd_perm)  20.7 us
    squeeze x16, local copies, waits for them, and re-layouts, run_stage(): x_left = lax.ppermute(x_run[-1], 'row', fwd_perm)  17.1 us
  transfers between devices with their start and end apart: 20, of which 16 were waited for; matrix products, arithmetic and copies ran while one was open for 1% of the time, Pallas kernels for 0%

commit v1 on v0

v1 whole, which is shorter than its diff:
```python
import jax
import jax.numpy as jnp
from jax import lax
from jax.experimental import pallas as pl
from jax.experimental.pallas import tpu as pltpu
from jax.sharding import PartitionSpec as P

SWEEPS = 4
TILE = 256
U, L, D = 0, 1, 2


def kernel(chain_len, d_hbm, l_hbm, u_hbm, f_hbm, x_hbm, o_hbm,
           w, nat, xraw, ft, xt, rl, rr,
           w_sem, f_sem, x_sem, o_sem, fs_sem, fr_sem, bs_sem, br_sem):
    pos = lax.axis_index("row")
    rows, size, _ = d_hbm.shape
    tiles = size // TILE
    has_left, has_right = pos > 0, pos < chain_len - 1
    hbm = {U: u_hbm, L: l_hbm, D: d_hbm}

    def w_copy(kind, row):
        slot = kind * rows + row
        return pltpu.make_async_copy(hbm[kind].at[row], w.at[slot], w_sem.at[slot])

    def f_copy(row):
        return pltpu.make_async_copy(f_hbm.at[row], nat.at[row], f_sem.at[row])

    def x_copy(row):
        return pltpu.make_async_copy(x_hbm.at[row], xraw.at[row], x_sem.at[row])

    def o_copy(row):
        return pltpu.make_async_copy(nat.at[row], o_hbm.at[row], o_sem.at[row])

    def fwd_copy(k):
        return pltpu.make_async_remote_copy(
            src_ref=xt.at[rows - 1], dst_ref=rl.at[k], send_sem=fs_sem.at[k], recv_sem=fr_sem.at[k],
            device_id={"row": pos + 1}, device_id_type=pl.DeviceIdType.MESH)

    def back_copy(k):
        return pltpu.make_async_remote_copy(
            src_ref=xt.at[0], dst_ref=rr.at[k], send_sem=bs_sem.at[k], recv_sem=br_sem.at[k],
            device_id={"row": pos - 1}, device_id_type=pl.DeviceIdType.MESH)

    x_copy(0).start()
    for row in range(rows):
        if row + 1 < rows:
            x_copy(row + 1).start()
        f_copy(row).start()
        w_copy(U, row).start()
        if row > 0:
            w_copy(L, row).start()
        w_copy(D, row).start()
    w_copy(L, 0).start()

    barrier = pltpu.get_barrier_semaphore()

    @pl.when(has_left)
    def _():
        pl.semaphore_signal(barrier, inc=1, device_id={"row": pos - 1}, device_id_type=pl.DeviceIdType.MESH)

    @pl.when(has_right)
    def _():
        pl.semaphore_signal(barrier, inc=1, device_id={"row": pos + 1}, device_id_type=pl.DeviceIdType.MESH)

    pl.semaphore_wait(barrier, has_left.astype(jnp.int32) + has_right.astype(jnp.int32))

    def transpose_w(slot):
        for a in range(tiles):
            for b in range(a, tiles):
                ra, rb = pl.ds(a * TILE, TILE), pl.ds(b * TILE, TILE)
                upper = w[slot, ra, rb]
                if a == b:
                    w[slot, ra, rb] = upper.T
                else:
                    lower = w[slot, rb, ra]
                    w[slot, ra, rb] = lower.T
                    w[slot, rb, ra] = upper.T

    x_copy(0).wait()
    xt[0] = xraw[0].T.astype(jnp.bfloat16)

    @pl.when(has_left)
    def _():
        back_copy(0).start()

    @pl.when(jnp.logical_not(has_left))
    def _():
        for k in range(SWEEPS):
            rl[k] = jnp.zeros(rl.shape[1:], rl.dtype)

    @pl.when(jnp.logical_not(has_right))
    def _():
        for k in range(SWEEPS):
            rr[k] = jnp.zeros(rr.shape[1:], rr.dtype)

    def prep(row, kind):
        pltpu.make_async_copy(hbm[kind].at[row], w.at[kind * rows + row], w_sem.at[kind * rows + row]).wait()
        transpose_w(kind * rows + row)

    def prep_row(row, carry):
        f_copy(row).wait()
        ft[row] = nat[row].T

        @pl.when(row > 0)
        def _():
            x_copy(row).wait()
            xt[row] = xraw[row].T.astype(jnp.bfloat16)

        prep(row, U)
        prep(row, L)
        prep(row, D)
        return carry

    lax.fori_loop(0, rows, prep_row, 0)

    def product(x, slot):
        return jnp.dot(x, w[slot], preferred_element_type=jnp.float32)

    def sweep(k, last):
        for row in range(rows):
            if row == rows - 1:
                @pl.when(has_right)
                def _():
                    back_copy(k).wait_recv()
            right = rr[k] if row == rows - 1 else xt[row + 1]
            t = ft[row] - product(right, U * rows + row)
            if row == 0:
                @pl.when(has_left)
                def _():
                    fwd_copy(k).wait_recv()
            left = rl[k] if row == 0 else xt[row - 1]
            t = t - product(left, L * rows + row)
            x_new = product(t.astype(jnp.bfloat16), D * rows + row)
            if row == 0:
                @pl.when(has_left)
                def _():
                    back_copy(k).wait_send()
            if row == rows - 1 and not (isinstance(k, int) and k == 0):
                @pl.when(has_right & (k > 0))
                def _():
                    fwd_copy(k - 1).wait_send()
            xt[row] = x_new.astype(jnp.bfloat16)
            if row == 0 and not last:
                @pl.when(has_left)
                def _():
                    back_copy(k + 1).start()
            if row == rows - 1:
                @pl.when(has_right)
                def _():
                    fwd_copy(k).start()
            if last:
                nat[row] = x_new.T
                o_copy(row).start()

    def mid_sweep(k, carry):
        sweep(k, False)
        return carry

    lax.fori_loop(0, SWEEPS - 1, mid_sweep, 0)
    sweep(SWEEPS - 1, True)

    @pl.when(has_right)
    def _():
        fwd_copy(SWEEPS - 1).wait_send()

    for row in range(rows):
        o_copy(row).wait()


def solution(mesh):
    chain_len = mesh.shape["row"]
    mat_spec = P(("batch", "row"), None, None)
    vec_spec = P(("batch", "row"), None, "col")

    def device_fn(d_inv, l_blk, u_blk, rhs_blk, x_init):
        rows, size, cols = rhs_blk.shape
        any_spec = pl.BlockSpec(memory_space=pl.ANY)
        dma = pltpu.SemaphoreType.DMA
        return pl.pallas_call(
            lambda *refs: kernel(chain_len, *refs),
            out_shape=jax.ShapeDtypeStruct(rhs_blk.shape, jnp.float32),
            in_specs=[any_spec] * 5,
            out_specs=any_spec,
            scratch_shapes=[
                pltpu.VMEM((3 * rows, size, size), jnp.bfloat16),
                pltpu.VMEM((rows, size, cols), jnp.float32),
                pltpu.VMEM((rows, size, cols), jnp.float32),
                pltpu.VMEM((rows, cols, size), jnp.float32),
                pltpu.VMEM((rows, cols, size), jnp.bfloat16),
                pltpu.VMEM((SWEEPS, cols, size), jnp.bfloat16),
                pltpu.VMEM((SWEEPS, cols, size), jnp.bfloat16),
                dma((3 * rows,)), dma((rows,)), dma((rows,)), dma((rows,)),
                dma((SWEEPS,)), dma((SWEEPS,)), dma((SWEEPS,)), dma((SWEEPS,)),
            ],
            compiler_params=pltpu.CompilerParams(
                collective_id=0, has_side_effects=True, vmem_limit_bytes=60 * 1024 * 1024),
        )(d_inv, l_blk, u_blk, rhs_blk, x_init)

    return jax.shard_map(device_fn, mesh=mesh, in_specs=(mat_spec, mat_spec, mat_spec, vec_spec, vec_spec),
                         out_specs=vec_spec, check_vma=False)
```

time: 721 us -> 96.6 us (0.13)
  waiting for transfers between devices: 474 us -> 0 us
  matrix products: 183 us -> 0 us
  Pallas kernels: 0 us -> 92.7 us
  starting transfers between devices: 29.4 us -> 0 us
  local copies, waits for them, and re-layouts: 29.4 us -> 3.76 us
    ppermute x20 -> x0, waiting for transfers between devices: 474 us -> none  [the longest x16 474 us: run_stage(): x_left = lax.ppermute(x_run[-1], 'row', fwd_perm)]
    dot_general x48 -> x0, matrix products: 183 us -> none  [the longest x24 126 us: row_step(): jnp.dot(d_i, t_i.astype(jnp.bfloat16), preferred_element_type=jnp.float32)]
    pallas_call x0 -> x1, Pallas kernels: none -> 92.7 us  [device_fn(): pl.pallas_call(lambda *refs: kernel(chain_len, *refs), out_shape=jax.Shap...]
    ppermute x20 -> x0, starting transfers between devices: 29.4 us -> none  [the longest x16 20.7 us: run_stage(): x_left = lax.ppermute(x_run[-1], 'row', fwd_perm)]
    squeeze x20 -> x0, local copies, waits for them, and re-layouts: 20.3 us -> none  [the longest x16 17.1 us: run_stage(): x_left = lax.ppermute(x_run[-1], 'row', fwd_perm)]
  transfers between devices with their start and end apart: 20 -> 0, of which waited for: 16 -> 0; matrix products, arithmetic and copies ran while one was open for 1% -> 0% of each run, Pallas kernels for 0% -> 0%
where the time goes in v1:
time: 96.6 us; the launch traced here: 96.5 us
  Pallas kernels  92.7 us (96%)
  local copies, waits for them, and re-layouts  3.76 us (4%)
    pallas_call x1, Pallas kernels, device_fn(): pl.pallas_call(lambda *refs: kernel(chain_len, *refs), out_shape=jax.Shap...  92.7 us
    unnamed x1, local copies, waits for them, and re-layouts  3.76 us

profile of v1, /device:TPU:7, one launch (start us, length us, event | category | flops | bytes accessed | tf_op | source)
XLA Modules:
  0.0 96.5 jit_solution(15571454526515905273)
XLA Ops:
  0.0 92.7 %shard_map.55 = f32[6,1024,128]{2,1,0:T(8,128)} custom-call(bf16[6,1024,1024]{2,1,0:T(8,128)(2,1)} %refs_0_.1, bf16[6,1024,1024]{2,1,0:T(8,128)(2,1)} %refs_1_.1, bf16[6,1024,1024]{2,1,0:T(8,128)(2,1)} %refs_2_.1, f32[6,1024,128]{2,1,0:T(8,128)} %refs_3_.1, f32[6,1024,128]{2,1,0:T(8,128)} %refs_4_.1), custom_call_target="tpu_custom_call" | custom-call | tf_op jit(solution)/shard_map/pallas_call | solution.py:180
  92.7 3.8 %copy.7 = f32[6,1024,128]{2,1,0:T(8,128)} copy(f32[6,1024,128]{2,1,0:T(8,128)} %shard_map.55) | data formatting | bytes 6291456

commit v2 on v0

v2 whole, which is shorter than its diff:
```python
import jax
import jax.numpy as jnp
from jax import lax
from jax.experimental import pallas as pl
from jax.experimental.pallas import tpu as pltpu
from jax.sharding import PartitionSpec as P

SWEEPS = 4
TILE = 256
GROUPS = 2
MESH = pl.DeviceIdType.MESH
F32, BF16 = jnp.float32, jnp.bfloat16


def kernel(chain_len, d_hbm, l_hbm, u_hbm, f_hbm, x_hbm, out,
           wu, wl, wd, fraw, xraw, ft, st, tmp, tb, xt, rl, rr,
           u_sem, l_sem, d_sem, f_sem, x_sem, fs_sem, fr_sem, bs_sem, br_sem):
    pos = lax.axis_index("row")
    rows, size, _ = d_hbm.shape
    cols = xt.shape[1]
    gcols = cols // GROUPS
    tiles = size // TILE
    first, has_left, has_right = pos == 0, pos > 0, pos < chain_len - 1
    mid = chain_len // 2
    last_row = rows - 1
    everything = pl.ds(0, cols)

    def u_copy(row):
        return pltpu.make_async_copy(u_hbm.at[row], wu.at[row], u_sem.at[row])

    def l_copy(row):
        return pltpu.make_async_copy(l_hbm.at[row], wl.at[row], l_sem.at[row])

    def d_copy(row):
        return pltpu.make_async_copy(d_hbm.at[row], wd.at[row], d_sem.at[row])

    def f_copy(row):
        return pltpu.make_async_copy(f_hbm.at[row], fraw.at[row], f_sem.at[row])

    def x_copy(row):
        return pltpu.make_async_copy(x_hbm.at[row], xraw.at[row], x_sem.at[row])

    def group(g):
        return pl.ds(g * gcols, gcols)

    def fwd_copy(k, g):
        return pltpu.make_async_remote_copy(
            src_ref=xt.at[last_row, group(g)], dst_ref=rl.at[k, group(g)],
            send_sem=fs_sem.at[k, g], recv_sem=fr_sem.at[k, g],
            device_id={"row": pos + 1}, device_id_type=MESH)

    def back_copy(k, g):
        return pltpu.make_async_remote_copy(
            src_ref=xt.at[0, group(g)], dst_ref=rr.at[k, group(g)],
            send_sem=bs_sem.at[k, g], recv_sem=br_sem.at[k, g],
            device_id={"row": pos - 1}, device_id_type=MESH)

    def load_u(row):
        f_copy(row).start()
        if isinstance(row, int):
            if row + 1 < rows:
                x_copy(row + 1).start()
        else:
            @pl.when(row + 1 < rows)
            def _():
                x_copy(row + 1).start()
        u_copy(row).start()

    x_copy(0).start()
    load_u(0)
    d_copy(0).start()
    load_u(1)
    l_copy(1).start()

    barrier = pltpu.get_barrier_semaphore()

    @pl.when(has_left)
    def _():
        pl.semaphore_signal(barrier, inc=1, device_id={"row": pos - 1}, device_id_type=MESH)

    @pl.when(has_right)
    def _():
        pl.semaphore_signal(barrier, inc=1, device_id={"row": pos + 1}, device_id_type=MESH)

    pl.semaphore_wait(barrier, has_left.astype(jnp.int32) + has_right.astype(jnp.int32))

    @pl.when(jnp.logical_not(has_left))
    def _():
        for k in range(SWEEPS):
            rl[k] = jnp.zeros(rl.shape[1:], rl.dtype)

    @pl.when(jnp.logical_not(has_right))
    def _():
        for k in range(SWEEPS):
            rr[k] = jnp.zeros(rr.shape[1:], rr.dtype)

    x_copy(0).wait()
    xt[0] = xraw[0].T.astype(BF16)

    @pl.when(has_left)
    def _():
        for g in range(GROUPS):
            back_copy(0, g).start()

    def transpose(w, row):
        for a in range(tiles):
            for b in range(a, tiles):
                ra, rb = pl.ds(a * TILE, TILE), pl.ds(b * TILE, TILE)
                upper = w[row, ra, rb]
                if a == b:
                    w[row, ra, rb] = upper.T
                else:
                    lower = w[row, rb, ra]
                    w[row, ra, rb] = lower.T
                    w[row, rb, ra] = upper.T

    def nds(n):
        return pl.ds(n * TILE, TILE)

    def product(x, lead, r, w, row):
        acc = [None] * tiles
        half = size // 2
        for h in range(2):
            ks = pl.ds(h * half, half)
            xv = x[(*lead, r, ks)]
            for n in range(tiles):
                part = jnp.dot(xv, w[row, ks, nds(n)], preferred_element_type=F32)
                acc[n] = part if acc[n] is None else acc[n] + part
        return acc

    def u_product(row, x, lead, dst, lead_dst):
        acc = product(x, lead, everything, wu, row)
        for n in range(tiles):
            dst[(*lead_dst, everything, nds(n))] = ft[row, :, nds(n)] - acc[n]

    def prep_fx(row, has_next):
        f_copy(row).wait()
        ft[row] = fraw[row].T
        if has_next:
            x_copy(row + 1).wait()
            xt[row + 1] = xraw[row + 1].T.astype(BF16)

    def finish_row(row, r, out_row=None):
        acc = product(tb, (), r, wd, row)
        for n in range(tiles):
            xt[row, r, nds(n)] = acc[n].astype(BF16)
            if out_row is not None:
                out[out_row, nds(n), r] = acc[n].T

    def store_t(r, base, lead, acc):
        for n in range(tiles):
            tb[r, nds(n)] = (base[(*lead, r, nds(n))] - acc[n]).astype(BF16)

    def issue_after_u(row):
        @pl.when(row + 1 < rows)
        def _():
            l_copy(row + 1).start()

    def issue_after_l(row):
        @pl.when(row + 1 < rows)
        def _():
            d_copy(row + 1).start()

    def issue_after_d(row):
        @pl.when(row + 2 < rows)
        def _():
            load_u(row + 2)

        @pl.when(row + 2 == rows)
        def _():
            l_copy(0).start()

    @pl.when(first)
    def _():
        prep_fx(0, True)
        u_copy(0).wait()
        d_copy(1).start()
        transpose(wu, 0)
        d_copy(0).wait()
        load_u(2)
        transpose(wd, 0)
        u_product(0, xt, (1,), tmp, ())
        for n in range(tiles):
            tb[:, nds(n)] = tmp[:, nds(n)].astype(BF16)

        def load_row(row, carry, has_next=True):
            prep_fx(row, has_next)
            u_copy(row).wait()
            issue_after_u(row)
            finish_row(row - 1, everything)
            transpose(wu, row)
            l_copy(row).wait()
            issue_after_l(row)
            if has_next:
                u_product(row, xt, (row + 1,), tmp, ())
            else:
                for g in range(GROUPS):
                    back_copy(0, g).wait_recv()
                u_product(row, rr, (0,), tmp, ())
            transpose(wl, row)
            d_copy(row).wait()
            issue_after_d(row)
            store_t(everything, tmp, (), product(xt, (row - 1,), everything, wl, row))
            transpose(wd, row)
            return carry

        lax.fori_loop(1, last_row, load_row, 0)
        load_row(last_row, 0, False)
        finish_row(last_row, everything)
        for g in range(GROUPS):
            fwd_copy(0, g).start()
        l_copy(0).wait()
        transpose(wl, 0)

        def u_pass(row, carry):
            u_product(row, xt, (row + 1,), st, (row,))
            return carry

        lax.fori_loop(0, last_row, u_pass, 0)

    @pl.when(jnp.logical_not(first))
    def _():
        prep_fx(0, True)
        u_copy(0).wait()
        d_copy(1).start()
        transpose(wu, 0)
        d_copy(0).wait()
        load_u(2)
        u_product(0, xt, (1,), st, (0,))
        transpose(wd, 0)

        def load_row(row, carry, has_next=True):
            prep_fx(row, has_next)
            u_copy(row).wait()
            issue_after_u(row)
            transpose(wu, row)
            l_copy(row).wait()
            issue_after_l(row)
            if has_next:
                u_product(row, xt, (row + 1,), st, (row,))
            transpose(wl, row)
            d_copy(row).wait()
            issue_after_d(row)
            transpose(wd, row)
            return carry

        lax.fori_loop(1, last_row, load_row, 0)
        load_row(last_row, 0, False)
        l_copy(0).wait()
        transpose(wl, 0)

    def sweep(k, last):
        def out_row(row):
            return row if last else None

        def recv_left(g):
            fwd_copy(k, g).wait_recv()

        def recv_right(g):
            back_copy(k, g).wait_recv()

        def send_left(g):
            if not last:
                back_copy(k + 1, g).start()

        @pl.when(pos == mid)
        def _():
            for g in range(GROUPS):
                recv_left(g)
                store_t(group(g), st, (0,), product(rl, (k,), group(g), wl, 0))
                back_copy(k, g).wait_send()
                finish_row(0, group(g), out_row(0))
                send_left(g)

        @pl.when(pos != mid)
        def _():
            @pl.when(has_left)
            def _():
                for g in range(GROUPS):
                    recv_left(g)
                    back_copy(k, g).wait_send()
            store_t(everything, st, (0,), product(rl, (k,), everything, wl, 0))
            finish_row(0, everything, out_row(0))

            @pl.when(has_left)
            def _():
                for g in range(GROUPS):
                    send_left(g)

        for row in range(1, last_row):
            store_t(everything, st, (row,), product(xt, (row - 1,), everything, wl, row))
            finish_row(row, everything, out_row(row))

        acc = product(xt, (last_row - 1,), everything, wl, last_row)
        for n in range(tiles):
            tmp[:, nds(n)] = ft[last_row, :, nds(n)] - acc[n]

        def wait_sent(g):
            if last:
                fwd_copy(k - 1, g).wait_send()
            else:
                @pl.when(k > 0)
                def _():
                    fwd_copy(k - 1, g).wait_send()

        @pl.when(pos == mid - 1)
        def _():
            for g in range(GROUPS):
                wait_sent(g)
            for g in range(GROUPS):
                recv_right(g)
                store_t(group(g), tmp, (), product(rr, (k,), group(g), wu, last_row))
                finish_row(last_row, group(g), out_row(last_row))
                fwd_copy(k, g).start()

        @pl.when(pos != mid - 1)
        def _():
            @pl.when(has_right)
            def _():
                for g in range(GROUPS):
                    wait_sent(g)
                    recv_right(g)
            store_t(everything, tmp, (), product(rr, (k,), everything, wu, last_row))
            finish_row(last_row, everything, out_row(last_row))

            @pl.when(has_right)
            def _():
                for g in range(GROUPS):
                    fwd_copy(k, g).start()

        if not last:
            for row in range(last_row):
                u_product(row, xt, (row + 1,), st, (row,))

    def mid_sweep(k, carry):
        sweep(k, False)
        return carry

    lax.fori_loop(first.astype(jnp.int32), SWEEPS - 1, mid_sweep, 0)
    sweep(SWEEPS - 1, True)

    @pl.when(has_right)
    def _():
        for g in range(GROUPS):
            fwd_copy(SWEEPS - 1, g).wait_send()


def solution(mesh):
    chain_len = mesh.shape["row"]
    mat_spec = P(("batch", "row"), None, None)
    vec_spec = P(("batch", "row"), None, "col")

    def device_fn(d_inv, l_blk, u_blk, rhs_blk, x_init):
        rows, size, cols = rhs_blk.shape
        any_spec = pl.BlockSpec(memory_space=pl.ANY)
        dma = pltpu.SemaphoreType.DMA
        return pl.pallas_call(
            lambda *refs: kernel(chain_len, *refs),
            out_shape=pltpu.VMEM(rhs_blk.shape, F32),
            in_specs=[any_spec] * 5,
            out_specs=pl.BlockSpec(memory_space=pltpu.VMEM),
            scratch_shapes=[
                pltpu.VMEM((rows, size, size), BF16),
                pltpu.VMEM((rows, size, size), BF16),
                pltpu.VMEM((rows, size, size), BF16),
                pltpu.VMEM((rows, size, cols), F32),
                pltpu.VMEM((rows, size, cols), F32),
                pltpu.VMEM((rows, cols, size), F32),
                pltpu.VMEM((rows, cols, size), F32),
                pltpu.VMEM((cols, size), F32),
                pltpu.VMEM((cols, size), BF16),
                pltpu.VMEM((rows, cols, size), BF16),
                pltpu.VMEM((SWEEPS, cols, size), BF16),
                pltpu.VMEM((SWEEPS, cols, size), BF16),
                dma((rows,)), dma((rows,)), dma((rows,)), dma((rows,)), dma((rows,)),
                dma((SWEEPS, GROUPS)), dma((SWEEPS, GROUPS)), dma((SWEEPS, GROUPS)), dma((SWEEPS, GROUPS)),
            ],
            compiler_params=pltpu.CompilerParams(
                collective_id=0, has_side_effects=True, vmem_limit_bytes=57 * 1024 * 1024),
        )(d_inv, l_blk, u_blk, rhs_blk, x_init)

    return jax.shard_map(device_fn, mesh=mesh, in_specs=(mat_spec, mat_spec, mat_spec, vec_spec, vec_spec),
                         out_specs=vec_spec, check_vma=False)
```

time: 721 us -> 69.3 us (0.10)
  waiting for transfers between devices: 474 us -> 0 us
  matrix products: 183 us -> 0 us
  Pallas kernels: 0 us -> 67.6 us
  starting transfers between devices: 29.4 us -> 0 us
  local copies, waits for them, and re-layouts: 29.4 us -> 1.67 us
    ppermute x20 -> x0, waiting for transfers between devices: 474 us -> none  [the longest x16 474 us: run_stage(): x_left = lax.ppermute(x_run[-1], 'row', fwd_perm)]
    dot_general x48 -> x0, matrix products: 183 us -> none  [the longest x24 126 us: row_step(): jnp.dot(d_i, t_i.astype(jnp.bfloat16), preferred_element_type=jnp.float32)]
    pallas_call x0 -> x1, Pallas kernels: none -> 67.6 us  [device_fn(): pl.pallas_call(lambda *refs: kernel(chain_len, *refs), out_shape=pltpu.VM...]
    ppermute x20 -> x0, starting transfers between devices: 29.4 us -> none  [the longest x16 20.7 us: run_stage(): x_left = lax.ppermute(x_run[-1], 'row', fwd_perm)]
    squeeze x20 -> x0, local copies, waits for them, and re-layouts: 20.3 us -> none  [the longest x16 17.1 us: run_stage(): x_left = lax.ppermute(x_run[-1], 'row', fwd_perm)]
  transfers between devices with their start and end apart: 20 -> 0, of which waited for: 16 -> 0; matrix products, arithmetic and copies ran while one was open for 1% -> 0% of each run, Pallas kernels for 0% -> 0%
where the time goes in v2:
time: 69.3 us
  Pallas kernels  67.6 us (98%)
  local copies, waits for them, and re-layouts  1.67 us (2%)
    pallas_call x1, Pallas kernels, device_fn(): pl.pallas_call(lambda *refs: kernel(chain_len, *refs), out_shape=pltpu.VM...  67.6 us
    unnamed x1, local copies, waits for them, and re-layouts  1.67 us

profile of v2, /device:TPU:7, one launch (start us, length us, event | category | flops | bytes accessed | tf_op | source)
XLA Modules:
  0.0 69.3 jit_solution(4665383501590070942)
XLA Ops:
  0.0 67.6 %shard_map.55 = f32[6,1024,128]{2,1,0:T(8,128)S(1)} custom-call(bf16[6,1024,1024]{2,1,0:T(8,128)(2,1)} %refs_0_.1, bf16[6,1024,1024]{2,1,0:T(8,128)(2,1)} %refs_1_.1, bf16[6,1024,1024]{2,1,0:T(8,128)(2,1)} %refs_2_.1, f32[6,1024,128]{2,1,0:T(8,128)} %refs_3_.1, f32[6,1024,128]{2,1,0:T(8,128)} %refs_4_.1), custom_call_target="tpu_custom_call" | custom-call | tf_op jit(solution)/shard_map/pallas_call | solution.py:357
  67.6 1.7 %copy.7 = f32[6,1024,128]{2,1,0:T(8,128)} copy(f32[6,1024,128]{2,1,0:T(8,128)S(1)} %shard_map.55) | data formatting | bytes 6291456
